TPU v7x, 32 devices: a whole 2x2x4 slice. The times are simulated.
32 devices in a mesh: dom: 16 (over z, y, core), ch: 2 (over x).
Axes of the slice: x: 2, y: 2, z: 4, core: 2. Of those that a mesh axis runs over, the one named last changes fastest.
Arguments:
- node_irreps: bfloat16 [49, 128, 256], P(None, 'ch', 'dom'), may hold values from -6 to 6
- out_grad: bfloat16 [49, 128, 256], P(None, 'ch', 'dom'), may hold values from -6 to 6
- edge_source: int32 [8, 256], P(None, 'dom'), may hold values from 0 to 31
- edge_rotation: int32 [8, 256], P(None, 'dom'), may hold values from 0 to 255
- edge_count: int32 [256], P('dom'), may hold values from 1 to 8
- ghost_slot: int32 [256], P('dom'), may hold values from 0 to 15, as said below
- wigner: float32 [455, 4096], P(None, 'dom'), may hold values from -1 to 1, as said below
- so2_m0: bfloat16 [7, 128, 7, 128], P(None, 'ch'), may hold values from -0.1875 to 0.1875
- so2_m1: bfloat16 [2, 6, 128, 6, 128], P(None, None, 'ch'), may hold values from -0.15625 to 0.15625
- so2_m2: bfloat16 [2, 5, 128, 5, 128], P(None, None, 'ch'), may hold values from -0.15625 to 0.15625
- attn_vector: float32 [128], P('ch'), may hold values from -60 to 60
Outputs:
- updated: bfloat16 [49, 128, 256], P(None, 'ch', 'dom')
- irreps_grad: float32 [49, 128, 256], P(None, 'ch', 'dom')
Inputs may be any that keep to these rules, and one draw needn't show every extreme that they name: `edge_source`: slots below 16 are the domain's own atoms in order; slot 16 + g is the domain's ghost g. `edge_rotation`: picks one of the 256 columns of wigner that belong to the atom's domain. Slots j < edge_count[a] are live, the others padding. `ghost_slot`: of a domain's 16 entries, the first 8 name atoms of the previous domain (cyclically) among its last 16 slots, the others atoms of the next domain among its first 16 slots. `wigner`: each column holds for l = 0..6 an orthogonal (2l+1) x (2l+1) block, row-major, blocks in order of l.
All inputs are finite; a program needn't handle non-finite values.
Results may differ from a plain program's by a relative error of at most 0.012.
The roundings to bfloat16 on the way count: a program that leaves them out, or rounds other values in their place, can miss the bound.
Values may be sent and summed in bfloat16 or wider, within the bound.
No kernel may reach another device: no remote copies, remote signals or barrier semaphores. Data moves between devices by JAX's collectives and lax.ppermute only.
A program may use at most 128 MiB of HBM per device.

v0:
```python
import functools

import jax
import jax.numpy as jnp
from jax import lax
from jax.experimental import pallas as pl
from jax.experimental.pallas import tpu as pltpu
from jax.sharding import PartitionSpec as P

HEADS = 8
LMAX = 6
MMAX = 2
F32 = jnp.float32
BF16 = jnp.bfloat16
HIGH = lax.Precision.HIGHEST
NT = (((1,), (1,)), ((), ()))
NN = (((1,), (0,)), ((), ()))


def dot(a, b, dims=NN, precision=None):
    return lax.dot_general(a, b, dims, precision=precision, preferred_element_type=F32)


def kept_rows():
    rows = {}
    place = 0
    offset = 0
    for level in range(LMAX + 1):
        width = 2 * level + 1
        reach = min(level, MMAX)
        for order in range(-reach, reach + 1):
            rows[level, order] = (place, offset + (level + order) * width, width)
            place += width
        offset += width * width
    return rows, place


ROWS, N_ROWS = kept_rows()
GROUPS = ((0, 0), (1, 1), (1, -1), (2, 2), (2, -2))


def plane_index():
    index = {}
    for least, order in GROUPS:
        for level in range(least, LMAX + 1):
            index[level, order] = len(index)
    return index


PLANES = plane_index()
K = (LMAX + 1) ** 2


def vmem(n):
    return [pl.BlockSpec(memory_space=pltpu.VMEM)] * n


def params(mib):
    return pltpu.CompilerParams(vmem_limit_bytes=mib * 1024 * 1024)


def column(table, slots, atoms):
    edges = slots * atoms
    row = lax.broadcasted_iota(jnp.int32, (edges, slots), 0)
    col = lax.broadcasted_iota(jnp.int32, (edges, slots), 1)
    pick = ((row >= col * atoms) & (row < (col + 1) * atoms)).astype(F32)
    spread = dot(pick, table.astype(F32), precision=HIGH)
    row = lax.broadcasted_iota(jnp.int32, (edges, atoms), 0)
    col = lax.broadcasted_iota(jnp.int32, (edges, atoms), 1)
    return jnp.sum(jnp.where(lax.rem(row, atoms) == col, spread, 0.0), axis=1, keepdims=True)


def onehot(values, width):
    edges = values.shape[0]
    lanes = lax.broadcasted_iota(jnp.int32, (edges, width), 1).astype(F32)
    return jnp.where(lanes == values, 1.0, 0.0).astype(F32)


def merge_kernel(shards, *refs):
    mine, others, full = refs[0], refs[1:-1], refs[-1]
    group = mine.shape[2]
    me = lax.axis_index("ch")
    pieces = [mine[...]] + [ref[...] for ref in others]
    for chunk in range(shards):
        value = pieces[0]
        for step in range(1, shards):
            value = jnp.where(lax.rem(me + step, shards) == chunk, pieces[step], value)
        full[:, :, chunk * group : (chunk + 1) * group] = value


def table_kernel(wigner, rotation, out_grad, dtab, g0, g1, g2, g3, g4, turned):
    slots, atoms = rotation.shape
    pick = onehot(column(rotation[...], slots, atoms), wigner.shape[1]).astype(BF16)
    wig = wigner[...]
    high = wig.astype(BF16)
    rest = wig - high.astype(F32)
    mid = rest.astype(BF16)
    low = (rest - mid.astype(F32)).astype(BF16)
    turned[...] = dot(pick, high, NT) + dot(pick, mid, NT) + dot(pick, low, NT)
    group = out_grad.shape[2]
    lanes = dtab.shape[2]
    outs = (g0, g1, g2, g3, g4)

    def step(slot, carry):
        here = pl.ds(pl.multiple_of(slot * atoms, atoms), atoms)
        mine = turned[here, :]
        for which, (least, order) in enumerate(GROUPS):
            parts = []
            for level in range(least, LMAX + 1):
                place, first, width = ROWS[level, order]
                acc = None
                for col in range(width):
                    entry = jnp.broadcast_to(mine[:, first + col : first + col + 1], (atoms, lanes))
                    dtab[place + col, here, :] = entry
                    term = entry[:, :group] * out_grad[level * level + col].astype(F32)
                    acc = term if acc is None else acc + term
                parts.append(acc)
            outs[which][here, :] = jnp.concatenate(parts, axis=1)
        return carry

    lax.fori_loop(0, slots, step, 0)


def rotate_in(slot, atoms, feats, dtab, rot):
    here = pl.ds(pl.multiple_of(slot * atoms, atoms), atoms)
    for level in range(LMAX + 1):
        width = 2 * level + 1
        planes = [feats[level * level + col, here, :] for col in range(width)]
        reach = min(level, MMAX)
        for order in range(-reach, reach + 1):
            place = ROWS[level, order][0]
            acc = dtab[place, here, :] * planes[0]
            for col in range(1, width):
                acc = acc + dtab[place + col, here, :] * planes[col]
            rot[PLANES[level, order], here, :] = acc.astype(BF16)


def rotate_out(slot, atoms, load, dtab, store):
    here = pl.ds(pl.multiple_of(slot * atoms, atoms), atoms)
    for level in range(LMAX + 1):
        width = 2 * level + 1
        reach = min(level, MMAX)
        orders = range(-reach, reach + 1)
        planes = {order: load(level, order, here) for order in orders}
        for col in range(width):
            acc = None
            for order in orders:
                term = dtab[ROWS[level, order][0] + col, here, :] * planes[order]
                acc = term if acc is None else acc + term
            store(level * level + col, here, acc)


def side(array, axis):
    return jnp.concatenate(array, axis=axis)


def edge_kernel(
    full, lower, upper, source, ghost, counts, dtab, g0, g1, g2, g3, g4, w0, w1, w2, attn,
    heads_here,
    own_out, prev_out, next_out, v0, v1, v2, v3, v4,
    feats, rot, drot, dfeats,
):
    slots, atoms = source.shape
    edges = slots * atoms
    chans = full.shape[2]
    group = w0.shape[2]
    half = ghost.shape[1] // 2
    slot_pick = onehot(column(source[...], slots, atoms), atoms + 2 * half).astype(BF16)
    row = lax.broadcasted_iota(jnp.int32, (2 * half, 2 * half), 0)
    col = lax.broadcasted_iota(jnp.int32, (2 * half, 2 * half), 1)
    ghosts = jnp.sum(jnp.where(row == col, ghost[...].astype(F32), 0.0), axis=1, keepdims=True)
    rows = lax.broadcasted_iota(jnp.int32, (2 * half, 1), 0)
    ghosts = ghosts + jnp.where(rows < half, atoms, 2 * atoms).astype(F32)
    own_row = lax.broadcasted_iota(jnp.int32, (atoms, 1), 0).astype(F32)
    places = onehot(side([own_row, ghosts], 0), 3 * atoms).astype(BF16)
    pick32 = dot(slot_pick, places)
    pick = pick32.astype(BF16)
    pick_back = jnp.transpose(pick32).astype(BF16)

    for first in range(0, K, 2):
        ks = [k for k in (first, first + 1) if k < K]
        table = side([side([full[k], lower[k], upper[k]], 0) for k in ks], 1)
        got = dot(pick, table)
        for at, k in enumerate(ks):
            feats[k] = got[:, at * chans : (at + 1) * chans]

    def in_step(slot, carry):
        rotate_in(slot, atoms, feats, dtab, rot)
        return carry

    lax.fori_loop(0, slots, in_step, 0)

    def planes_of(which):
        least, order = GROUPS[which]
        return side([rot[PLANES[level, order]] for level in range(least, LMAX + 1)], 1)

    def weights_of(ref):
        count = ref.shape[-3]
        lead = ref.shape[-2] * count * (ref.shape[0] if len(ref.shape) == 5 else 1)
        if len(ref.shape) == 4:
            parts = [ref[:, level].reshape(lead, chans) for level in range(count)]
        else:
            parts = [ref[:, :, level].reshape(lead, chans) for level in range(count)]
        return side(parts, 1)

    y0 = dot(planes_of(0), weights_of(w0), NT)

    def mixed(which, ref):
        both = dot(side([planes_of(which), planes_of(which + 1)], 0), weights_of(ref), NT)
        wide = both.shape[1] // 2
        plus = both[:edges, :wide] - both[edges:, wide:]
        minus = both[edges:, :wide] + both[:edges, wide:]
        return plus, minus

    y1, y2 = mixed(1, w1)
    y3, y4 = mixed(3, w2)
    mixes = (y0, y1, y2, y3, y4)
    grads = (g0[...], g1[...], g2[...], g3[...], g4[...])

    scalar = y0[:, :group]
    sig = 1.0 / (1.0 + jnp.exp(-scalar))
    width = group // heads_here
    head_row = lax.broadcasted_iota(jnp.int32, (group, group), 0) // width
    head_col = lax.broadcasted_iota(jnp.int32, (group, group), 1) // width
    same_head = jnp.where(head_row == head_col, 1.0, 0.0).astype(F32)
    vector = attn[...]
    silu = scalar * sig
    score = dot(silu * vector, same_head, precision=HIGH).reshape(slots, atoms, group)
    cnt = jnp.broadcast_to(counts[...], (slots, atoms))
    slot_no = lax.broadcasted_iota(jnp.int32, (slots, atoms), 0)
    live = (column(slot_no < cnt, slots, atoms) > 0.5)
    live = jnp.broadcast_to(live, (edges, group)).reshape(slots, atoms, group)
    score = jnp.where(live, score, -1e30)
    top = jnp.max(score, axis=0, keepdims=True)
    weight = jnp.where(live, jnp.exp(score - top), 0.0)
    weight = weight / jnp.sum(weight, axis=0, keepdims=True)
    flat = weight.reshape(edges, group)
    factor = flat * sig

    overlap = None
    for grad, mix in zip(grads, mixes):
        both = grad * mix
        for at in range(0, both.shape[1], group):
            piece = both[:, at : at + group]
            overlap = piece if overlap is None else overlap + piece
    dweight = dot(overlap * sig, same_head, precision=HIGH).reshape(slots, atoms, group)
    mean = jnp.sum(weight * dweight, axis=0, keepdims=True)
    dscore = (weight * (dweight - mean)).reshape(edges, group)
    dscalar = overlap * factor * (1.0 - sig) + dscore * vector * sig * (1.0 + scalar * (1.0 - sig))

    dmix = []
    for grad, mix, out in zip(grads, mixes, (v0, v1, v2, v3, v4)):
        wide = side([factor] * (mix.shape[1] // group), 1)
        out[...] = mix * wide
        dmix.append(grad * wide)
    head = dmix[0][:, :group] + dscalar
    back0 = side([head, dmix[0][:, group:]], 1).astype(BF16)

    def keep(which, value, first=0):
        least, order = GROUPS[which]
        for at, level in enumerate(range(least, LMAX + 1)):
            drot[PLANES[level, order]] = (
                value[:, at * chans : (at + 1) * chans].astype(BF16).astype(F32)
            )

    keep(0, dot(back0, weights_of(w0)))
    for which, ref in ((1, w1), (3, w2)):
        plus, minus = dmix[which], dmix[which + 1]
        stacked = side([side([plus, minus], 1), side([minus, -plus], 1)], 0).astype(BF16)
        both = dot(stacked, weights_of(ref))
        keep(which, both[:edges])
        keep(which + 1, both[edges:])

    def load(level, order, here):
        return drot[PLANES[level, order], here, :]

    def store(k, here, value):
        dfeats[k, here, :] = value.astype(BF16)

    def out_step(slot, carry):
        rotate_out(slot, atoms, load, dtab, store)
        return carry

    lax.fori_loop(0, slots, out_step, 0)

    for first in range(0, K, 2):
        ks = [k for k in (first, first + 1) if k < K]
        got = dot(pick_back, side([dfeats[k] for k in ks], 1))
        for at, k in enumerate(ks):
            mine = got[:, at * chans : (at + 1) * chans]
            own_out[k] = mine[:atoms]
            prev_out[k] = mine[atoms : 2 * atoms].astype(BF16)
            next_out[k] = mine[2 * atoms :].astype(BF16)


def update_kernel(v0, v1, v2, v3, v4, dtab, mine, out, agg):
    atoms, group = mine.shape[1], mine.shape[2]
    slots = dtab.shape[1] // atoms
    values = (v0, v1, v2, v3, v4)
    lanes = dtab.shape[2]
    agg[...] = jnp.zeros_like(agg)

    def step(slot, carry):
        here = pl.ds(pl.multiple_of(slot * atoms, atoms), atoms)
        wide = [ref[here, :] for ref in values]
        for level in range(LMAX + 1):
            reach = min(level, MMAX)
            planes = {}
            for which, (least, order) in enumerate(GROUPS):
                if least <= level:
                    at = (level - least) * group
                    planes[order] = wide[which][:, at : at + group]
            for col in range(2 * level + 1):
                acc = agg[level * level + col]
                for order in range(-reach, reach + 1):
                    entry = dtab[ROWS[level, order][0] + col, here, :]
                    acc = acc + entry[:, :group] * planes[order]
                agg[level * level + col] = acc
        return carry

    lax.fori_loop(0, slots, step, 0)
    out[...] = (mine[...].astype(F32) + agg[...]).astype(BF16)


def settle_kernel(shards, own, above, below, out_grad, mine_out, *others):
    group = out_grad.shape[2]
    me = lax.axis_index("ch")
    total = own[...] + above[...].astype(F32) + below[...].astype(F32)
    for step in range(shards):
        wanted = lax.rem(me + step, shards)
        value = total[:, :, :group]
        for chunk in range(1, shards):
            value = jnp.where(wanted == chunk, total[:, :, chunk * group : (chunk + 1) * group], value)
        if step == 0:
            mine_out[...] = value + out_grad[...].astype(F32)
        else:
            others[step - 1][...] = value.astype(BF16)


def shift(array, axis, by):
    count = lax.axis_size(axis)
    return lax.ppermute(array, axis, [(i, (i + by) % count) for i in range(count)])


def cost(flops, size):
    return pl.CostEstimate(flops=flops, bytes_accessed=size, transcendentals=0)


def on_device(
    node_irreps, out_grad, edge_source, edge_rotation, edge_count, ghost_slot, wigner,
    so2_m0, so2_m1, so2_m2, attn_vector,
):
    group, atoms = node_irreps.shape[1], node_irreps.shape[2]
    shards = lax.axis_size("ch")
    chans = group * shards
    slots = edge_source.shape[0]
    edges = slots * atoms
    heads_here = HEADS // shards
    shape = jax.ShapeDtypeStruct
    mine = jnp.transpose(node_irreps, (0, 2, 1))
    grad = jnp.transpose(out_grad, (0, 2, 1))
    w0 = jnp.transpose(so2_m0, (0, 2, 1, 3))
    w1 = jnp.transpose(so2_m1, (0, 1, 3, 2, 4))
    w2 = jnp.transpose(so2_m2, (0, 1, 3, 2, 4))

    others = [shift(mine, "ch", -step) for step in range(1, shards)]
    full = pl.pallas_call(
        functools.partial(merge_kernel, shards),
        out_shape=shape((K, atoms, chans), BF16),
        in_specs=vmem(shards),
        out_specs=vmem(1)[0],
        compiler_params=params(4),
        name="merge",
    )(mine, *others)
    lower = shift(full, "dom", 1)
    upper = shift(full, "dom", -1)

    widths = [(LMAX + 1 - least) * group for least, _ in GROUPS]
    dtab, *grads = pl.pallas_call(
        table_kernel,
        out_shape=[shape((N_ROWS, edges, chans), F32)] + [shape((edges, w), F32) for w in widths],
        in_specs=vmem(3),
        out_specs=vmem(6),
        scratch_shapes=[pltpu.VMEM((edges, wigner.shape[0]), F32)],
        compiler_params=params(24),
        cost_estimate=cost(50_000_000, 16_000_000),
        name="tables",
    )(wigner, edge_rotation, grad)

    body = lambda *refs: edge_kernel(*refs[:16], heads_here, *refs[16:])
    own, to_prev, to_next, *values = pl.pallas_call(
        body,
        out_shape=[
            shape((K, atoms, chans), F32),
            shape((K, atoms, chans), BF16),
            shape((K, atoms, chans), BF16),
        ] + [shape((edges, w), F32) for w in widths],
        in_specs=vmem(16),
        out_specs=vmem(8),
        scratch_shapes=[
            pltpu.VMEM((K, edges, chans), F32),
            pltpu.VMEM((len(PLANES), edges, chans), BF16),
            pltpu.VMEM((len(PLANES), edges, chans), F32),
            pltpu.VMEM((K, edges, chans), BF16),
        ],
        compiler_params=params(40),
        cost_estimate=cost(2_000_000_000, 20_000_000),
        name="edges",
    )(
        full, lower, upper, edge_source, ghost_slot.reshape(1, -1), edge_count.reshape(1, -1),
        dtab, *grads, w0, w1, w2, attn_vector.reshape(1, -1),
    )
    above = shift(to_prev, "dom", -1)
    below = shift(to_next, "dom", 1)

    updated = pl.pallas_call(
        update_kernel,
        out_shape=shape((K, atoms, group), BF16),
        in_specs=vmem(7),
        out_specs=vmem(1)[0],
        scratch_shapes=[pltpu.VMEM((K, atoms, group), F32)],
        compiler_params=params(24),
        cost_estimate=cost(20_000_000, 16_000_000),
        name="update",
    )(*values, dtab, mine)

    mine_grad, *sent = pl.pallas_call(
        functools.partial(settle_kernel, shards),
        out_shape=[shape((K, atoms, group), F32)] + [shape((K, atoms, group), BF16)] * (shards - 1),
        in_specs=vmem(4),
        out_specs=vmem(shards),
        compiler_params=params(8),
        name="settle",
    )(own, above, below, grad)
    for step in range(1, shards):
        mine_grad = mine_grad + shift(sent[step - 1], "ch", step).astype(F32)
    return (jnp.transpose(updated, (0, 2, 1)), jnp.transpose(mine_grad, (0, 2, 1)))


def solution(mesh):
    placed = (
        P(None, "ch", "dom"), P(None, "ch", "dom"), P(None, "dom"), P(None, "dom"), P("dom"),
        P("dom"), P(None, "dom"), P(None, "ch", None, None), P(None, None, "ch", None, None),
        P(None, None, "ch", None, None), P("ch"),
    )
    return jax.shard_map(
        on_device,
        mesh=mesh,
        in_specs=placed,
        out_specs=(P(None, "ch", "dom"), P(None, "ch", "dom")),
        check_vma=False,
    )
```

profile of v0, /device:TPU:0, one launch (start us, length us, event | category | flops | bytes accessed | tf_op | source)
XLA Modules:
  0.0 69.1 jit_solution(4466072050351021538)
XLA Ops:
  0.6 3.0 %collective-permute-start = (bf16[49,16,64]{2,1,0:T(8,128)(2,1)}, bf16[49,16,64]{2,1,0:T(8,128)(2,1)S(1)}, u32[]{:S(2)}, u32[]{:S(2)}) collective-permute-start(bf16[49,16,64]{2,1,0:T(8,128)(2,1)} %bitcast.16), channel_id=1, source_target_pairs={{0,1},{1,0},{2,3},{3,2},{4,5},{5,4},{6,7},{7,6},{8,9},{9,8},{10,11... | collective-permute-start | bytes 301064 | tf_op jit(solution)/shard_map/ppermute | solution.py:342
  3.7 5.2 %collective-permute-done.refs_1_ = bf16[49,16,64]{2,1,0:T(8,128)(2,1)S(1)} collective-permute-done((bf16[49,16,64]{2,1,0:T(8,128)(2,1)}, bf16[49,16,64]{2,1,0:T(8,128)(2,1)S(1)}, u32[]{:S(2)}, u32[]{:S(2)}) %collective-permute-start) | collective-permute-done | bytes 100384 | tf_op jit(solution)/shard_map/ppermute | solution.py:342
  8.9 0.9 %copy-done.7 = bf16[49,64,16]{1,2,0:T(8,128)(2,1)S(1)} copy-done((bf16[49,64,16]{1,2,0:T(8,128)(2,1)S(1)}, bf16[49,64,16]{1,2,0:T(8,128)(2,1)}, u32[]{:S(2)}) %copy-start.7) | copy-done | bytes 100376
  10.0 3.4 %collective-permute-start.2 = (bf16[49,16,128]{2,1,0:T(8,128)(2,1)S(1)}, bf16[49,16,128]{2,1,0:T(8,128)(2,1)S(1)}, u32[]{:S(2)}, u32[]{:S(2)}) collective-permute-start(bf16[49,16,128]{2,1,0:T(8,128)(2,1)S(1)} %merge.1.refs_0_), channel_id=1, source_target_pairs={{0,30},{2,0},{4,2},{6,4},{8,6},{10,8},{12,10},{14,12},{16,14},{18,... | collective-permute-start | bytes 602120 | tf_op jit(solution)/shard_map/ppermute | solution.py:342
  13.5 0.9 %copy-done.4 = bf16[49,64,16]{1,2,0:T(8,128)(2,1)S(1)} copy-done((bf16[49,64,16]{1,2,0:T(8,128)(2,1)S(1)}, bf16[49,64,16]{1,2,0:T(8,128)(2,1)}, u32[]{:S(2)}) %copy-start.4) | copy-done | bytes 100376
  14.4 1.0 %copy-done.9 = f32[455,256]{1,0:T(8,128)S(1)} copy-done((f32[455,256]{1,0:T(8,128)S(1)}, f32[455,256]{1,0:T(8,128)}, u32[]{:S(2)}) %copy-start.9) | copy-done | bytes 465944
  15.4 0.7 copy-done.10
  16.1 9.2 %tables.1 = (f32[235,128,128]{2,1,0:T(8,128)S(1)}, f32[128,448]{1,0:T(8,128)S(1)}, f32[128,384]{1,0:T(8,128)S(1)}, f32[128,384]{1,0:T(8,128)S(1)}, f32[128,320]{1,0:T(8,128)S(1)}, /*index=5*/f32[128,320]{1,0:T(8,128)S(1)}) custom-call(f32[455,256]{1,0:T(8,128)S(1)} %copy-done.9, s32[8,16]{1,0:T(8,128)S(1)} %copy-done.10, bf16[49,16,64]{2,1,0:T(8,128)(2,1)S(1)} %bitcast.13), custom_call_target="tpu_custom_call" | custom-call | flops 50000000 | bytes 16000000 | tf_op jit(solution)/shard_map/tables/pallas_call | solution.py:379
  25.3 5.4 %copy-done = f32[235,128,128]{2,1,0:T(8,128)} copy-done((f32[235,128,128]{2,1,0:T(8,128)}, f32[235,128,128]{2,1,0:T(8,128)S(1)}, u32[]{:S(2)}) %copy-start) | copy-done | bytes 15400984
  30.7 1.4 %copy-done.2 = bf16[2,6,64,6,128]{4,2,3,1,0:T(8,128)(2,1)S(1)} copy-done((bf16[2,6,64,6,128]{4,2,3,1,0:T(8,128)(2,1)S(1)}, bf16[2,6,64,6,128]{4,2,3,1,0:T(8,128)(2,1)}, u32[]{:S(2)}) %copy-start.2) | copy-done | bytes 1179672
  32.1 1.4 %copy-done.3 = bf16[2,5,64,5,128]{4,2,3,1,0:T(8,128)(2,1)S(1)} copy-done((bf16[2,5,64,5,128]{4,2,3,1,0:T(8,128)(2,1)S(1)}, bf16[2,5,64,5,128]{4,2,3,1,0:T(8,128)(2,1)}, u32[]{:S(2)}) %copy-start.3) | copy-done | bytes 819224
  33.5 1.5 %copy-done.6 = bf16[7,64,7,128]{3,1,2,0:T(8,128)(2,1)S(1)} copy-done((bf16[7,64,7,128]{3,1,2,0:T(8,128)(2,1)S(1)}, bf16[7,64,7,128]{3,1,2,0:T(8,128)(2,1)}, u32[]{:S(2)}) %copy-start.6) | copy-done | bytes 802840
  35.0 1.0 %copy-done.11 = s32[8,16]{1,0:T(8,128)S(1)} copy-done((s32[8,16]{1,0:T(8,128)S(1)}, s32[8,16]{1,0:T(8,128)}, u32[]{:S(2)}) %copy-start.11) | copy-done | bytes 536
  36.0 0.7 copy-done.12
  36.7 0.7 copy-done.13
  37.4 0.7 copy-done.14
  38.0 11.7 %edges.1 = (f32[49,16,128]{2,1,0:T(8,128)S(1)}, bf16[49,16,128]{2,1,0:T(8,128)(2,1)S(1)}, bf16[49,16,128]{2,1,0:T(8,128)(2,1)S(1)}, f32[128,448]{1,0:T(8,128)S(1...) custom-call(bf16[49,16,128]{2,1,0:T(8,128)(2,1)S(1)} %merge.1.refs_0_, ...), custom_call_target="tpu_custom_call" | custom-call | flops 2000000000 | bytes 20000000 | tf_op jit(solution)/shard_map/edges/pallas_call | solution.py:391
  49.7 4.5 %collective-permute-start.3 = (bf16[49,16,128]{2,1,0:T(8,128)(2,1)S(1)}, bf16[49,16,128]{2,1,0:T(8,128)(2,1)S(1)}, u32[]{:S(2)}, u32[]{:S(2)}) collective-permute-start(bf16[49,16,128]{2,1,0:T(8,128)(2,1)S(1)} %get-tuple-element.30), channel_id=1, source_target_pairs={{0,30},{2,0},{4,2},{6,4},{8,6},{10,8},{12,10},{14,12},{16,14},{18,... | collective-permute-start | bytes 602120 | tf_op jit(solution)/shard_map/ppermute | solution.py:342
  54.2 3.2 %collective-permute-done.3.above = bf16[49,16,128]{2,1,0:T(8,128)(2,1)S(1)} collective-permute-done((bf16[49,16,128]{2,1,0:T(8,128)(2,1)S(1)}, bf16[49,16,128]{2,1,0:T(8,128)(2,1)S(1)}, u32[]{:S(2)}, u32[]{:S(2)}) %collective-permute-start.3) | collective-permute-done | bytes 200736 | tf_op jit(solution)/shard_map/ppermute | solution.py:342
  57.4 4.6 %collective-permute-done.4.below = bf16[49,16,128]{2,1,0:T(8,128)(2,1)S(1)} collective-permute-done((bf16[49,16,128]{2,1,0:T(8,128)(2,1)S(1)}, bf16[49,16,128]{2,1,0:T(8,128)(2,1)S(1)}, u32[]{:S(2)}, u32[]{:S(2)}) %collective-permute-start.4) | collective-permute-done | bytes 200736 | tf_op jit(solution)/shard_map/ppermute | solution.py:342
  62.5 1.6 %collective-permute-start.5 = (bf16[49,16,64]{2,1,0:T(8,128)(2,1)S(1)}, bf16[49,16,64]{2,1,0:T(8,128)(2,1)S(1)}, u32[]{:S(2)}, u32[]{:S(2)}) collective-permute-start(bf16[49,16,64]{2,1,0:T(8,128)(2,1)S(1)} %get-tuple-element.33), channel_id=1, source_target_pairs={{0,1},{1,0},{2,3},{3,2},{4,5},{5,4},{6,7},{7,6},{8,9},{9,8},{10,11... | collective-permute-start | bytes 301064 | tf_op jit(solution)/shard_map/ppermute | solution.py:342
  64.1 2.8 %update.1 = bf16[49,16,64]{2,1,0:T(8,128)(2,1)} custom-call(f32[128,448]{1,0:T(8,128)S(1)} %get-tuple-element.24.v0, f32[128,384]{1,0:T(8,128)S(1)} %get-tuple-element.25.v1, f32[128,384]{1,0:T(8,128)S(1)} %get-tuple-element.26.v2, f32[128,320]{1,0:T(8,128)S(1)} %get-tuple-element.27.v3, f32[128,320]{1,0:T(8,128)S(1)} %get-tuple-element.28.v4, ...), custom_call_target="tpu_custom_call" | custom-call | flops 20000000 | bytes 16000000 | tf_op jit(solution)/shard_map/update/pallas_call | solution.py:416
  66.9 1.4 %collective-permute-done.5 = bf16[49,16,64]{2,1,0:T(8,128)(2,1)S(1)} collective-permute-done((bf16[49,16,64]{2,1,0:T(8,128)(2,1)S(1)}, bf16[49,16,64]{2,1,0:T(8,128)(2,1)S(1)}, u32[]{:S(2)}, u32[]{:S(2)}) %collective-permute-start.5) | collective-permute-done | bytes 100384 | tf_op jit(solution)/shard_map/ppermute | solution.py:342
  68.3 0.8 %add_bitcast_fusion = f32[49,64,16]{1,2,0:T(8,128)} fusion(f32[49,16,64]{2,1,0:T(8,128)S(1)} %get-tuple-element.32, bf16[49,16,64]{2,1,0:T(8,128)(2,1)S(1)} %collective-permute-done.5), kind=kLoop, calls=%fused_computation | loop fusion | flops 100352 | bytes 501760 | tf_op jit(solution)/shard_map/transpose | solution.py:437
  (24 shorter events, 0.7 us)
Async XLA Ops:
  0.6 61.4 %copy-start.5 = (bf16[49,64,16]{1,2,0:T(8,128)(2,1)S(1)}, bf16[49,64,16]{1,2,0:T(8,128)(2,1)}, u32[]{:S(2)}) copy-start(bf16[49,64,16]{1,2,0:T(8,128)(2,1)} %param.12) | copy-start | bytes 301060
  0.6 8.2 %collective-permute-start = (bf16[49,16,64]{2,1,0:T(8,128)(2,1)}, bf16[49,16,64]{2,1,0:T(8,128)(2,1)S(1)}, u32[]{:S(2)}, u32[]{:S(2)}) collective-permute-start(bf16[49,16,64]{2,1,0:T(8,128)(2,1)} %bitcast.16), channel_id=1, source_target_pairs={{0,1},{1,0},{2,3},{3,2},{4,5},{5,4},{6,7},{7,6},{8,9},{9,8},{10,11... | collective-permute-start | bytes 301064 | tf_op jit(solution)/shard_map/ppermute | solution.py:342
  8.9 0.9 %copy-start.7 = (bf16[49,64,16]{1,2,0:T(8,128)(2,1)S(1)}, bf16[49,64,16]{1,2,0:T(8,128)(2,1)}, u32[]{:S(2)}) copy-start(bf16[49,64,16]{1,2,0:T(8,128)(2,1)} %param.11) | copy-start | bytes 301060
  9.8 54.3 %copy-start.8 = (bf16[49,64,16]{1,2,0:T(8,128)(2,1)S(1)}, bf16[49,64,16]{1,2,0:T(8,128)(2,1)}, u32[]{:S(2)}) copy-start(bf16[49,64,16]{1,2,0:T(8,128)(2,1)} %param.11) | copy-start | bytes 301060
  10.0 20.7 %collective-permute-start.2 = (bf16[49,16,128]{2,1,0:T(8,128)(2,1)S(1)}, bf16[49,16,128]{2,1,0:T(8,128)(2,1)S(1)}, u32[]{:S(2)}, u32[]{:S(2)}) collective-permute-start(bf16[49,16,128]{2,1,0:T(8,128)(2,1)S(1)} %merge.1.refs_0_), channel_id=1, source_target_pairs={{0,30},{2,0},{4,2},{6,4},{8,6},{10,8},{12,10},{14,12},{16,14},{18,... | collective-permute-start | bytes 602120 | tf_op jit(solution)/shard_map/ppermute | solution.py:342
  13.5 17.2 %collective-permute-start.1 = (bf16[49,16,128]{2,1,0:T(8,128)(2,1)S(1)}, bf16[49,16,128]{2,1,0:T(8,128)(2,1)S(1)}, u32[]{:S(2)}, u32[]{:S(2)}) collective-permute-start(bf16[49,16,128]{2,1,0:T(8,128)(2,1)S(1)} %merge.1.refs_0_), channel_id=1, source_target_pairs={{0,2},{2,4},{4,6},{6,8},{8,10},{10,12},{12,14},{14,16},{16,18},{18... | collective-permute-start | bytes 602120 | tf_op jit(solution)/shard_map/ppermute | solution.py:342
  13.5 0.9 %copy-start.4 = (bf16[49,64,16]{1,2,0:T(8,128)(2,1)S(1)}, bf16[49,64,16]{1,2,0:T(8,128)(2,1)}, u32[]{:S(2)}) copy-start(bf16[49,64,16]{1,2,0:T(8,128)(2,1)} %param.12) | copy-start | bytes 301060
  14.4 1.0 %copy-start.9 = (f32[455,256]{1,0:T(8,128)S(1)}, f32[455,256]{1,0:T(8,128)}, u32[]{:S(2)}) copy-start(f32[455,256]{1,0:T(8,128)} %wigner.1) | copy-start | bytes 1397764
  15.4 0.7 copy-start.10
  25.3 5.4 %copy-start = (f32[235,128,128]{2,1,0:T(8,128)}, f32[235,128,128]{2,1,0:T(8,128)S(1)}, u32[]{:S(2)}) copy-start(f32[235,128,128]{2,1,0:T(8,128)S(1)} %get-tuple-element.18.refs_6_.dtab) | copy-start | bytes 46202884
  30.7 33.4 %copy-start.1 = (f32[235,128,128]{2,1,0:T(8,128)S(1)}, f32[235,128,128]{2,1,0:T(8,128)}, u32[]{:S(2)}) copy-start(f32[235,128,128]{2,1,0:T(8,128)} %copy-done) | copy-start | bytes 46202884
  30.7 1.4 %copy-start.2 = (bf16[2,6,64,6,128]{4,2,3,1,0:T(8,128)(2,1)S(1)}, bf16[2,6,64,6,128]{4,2,3,1,0:T(8,128)(2,1)}, u32[]{:S(2)}) copy-start(bf16[2,6,64,6,128]{4,2,3,1,0:T(8,128)(2,1)} %param.19) | copy-start | bytes 3538948
  32.1 1.4 %copy-start.3 = (bf16[2,5,64,5,128]{4,2,3,1,0:T(8,128)(2,1)S(1)}, bf16[2,5,64,5,128]{4,2,3,1,0:T(8,128)(2,1)}, u32[]{:S(2)}) copy-start(bf16[2,5,64,5,128]{4,2,3,1,0:T(8,128)(2,1)} %param.20) | copy-start | bytes 2457604
  33.5 1.5 %copy-start.6 = (bf16[7,64,7,128]{3,1,2,0:T(8,128)(2,1)S(1)}, bf16[7,64,7,128]{3,1,2,0:T(8,128)(2,1)}, u32[]{:S(2)}) copy-start(bf16[7,64,7,128]{3,1,2,0:T(8,128)(2,1)} %param.18) | copy-start | bytes 2408452
  35.0 1.0 %copy-start.11 = (s32[8,16]{1,0:T(8,128)S(1)}, s32[8,16]{1,0:T(8,128)}, u32[]{:S(2)}) copy-start(s32[8,16]{1,0:T(8,128)} %refs_3_.1) | copy-start | bytes 1540
  36.0 0.7 copy-start.12
  36.7 0.7 copy-start.13
  37.4 0.7 copy-start.14
  49.7 7.7 %collective-permute-start.3 = (bf16[49,16,128]{2,1,0:T(8,128)(2,1)S(1)}, bf16[49,16,128]{2,1,0:T(8,128)(2,1)S(1)}, u32[]{:S(2)}, u32[]{:S(2)}) collective-permute-start(bf16[49,16,128]{2,1,0:T(8,128)(2,1)S(1)} %get-tuple-element.30), channel_id=1, source_target_pairs={{0,30},{2,0},{4,2},{6,4},{8,6},{10,8},{12,10},{14,12},{16,14},{18,... | collective-permute-start | bytes 602120 | tf_op jit(solution)/shard_map/ppermute | solution.py:342
  54.2 7.8 %collective-permute-start.4 = (bf16[49,16,128]{2,1,0:T(8,128)(2,1)S(1)}, bf16[49,16,128]{2,1,0:T(8,128)(2,1)S(1)}, u32[]{:S(2)}, u32[]{:S(2)}) collective-permute-start(bf16[49,16,128]{2,1,0:T(8,128)(2,1)S(1)} %get-tuple-element.31), channel_id=1, source_target_pairs={{0,2},{2,4},{4,6},{6,8},{8,10},{10,12},{12,14},{14,16},{16,18},{18... | collective-permute-start | bytes 602120 | tf_op jit(solution)/shard_map/ppermute | solution.py:342
  62.5 5.8 %collective-permute-start.5 = (bf16[49,16,64]{2,1,0:T(8,128)(2,1)S(1)}, bf16[49,16,64]{2,1,0:T(8,128)(2,1)S(1)}, u32[]{:S(2)}, u32[]{:S(2)}) collective-permute-start(bf16[49,16,64]{2,1,0:T(8,128)(2,1)S(1)} %get-tuple-element.33), channel_id=1, source_target_pairs={{0,1},{1,0},{2,3},{3,2},{4,5},{5,4},{6,7},{7,6},{8,9},{9,8},{10,11... | collective-permute-start | bytes 301064 | tf_op jit(solution)/shard_map/ppermute | solution.py:342
where the time goes:
time: 69.4 us; the launch traced here: 69.1 us
  Pallas kernels  24.3 us (35%)
  local copies, waits for them, and re-layouts  16.3 us (23%)
  waiting for transfers between devices  14.4 us (21%)
  starting transfers between devices  12.5 us (18%)
  other arithmetic  0.8 us (1%)
    unnamed x30, local copies, waits for them, and re-layouts  16.3 us
    ppermute x6, waiting for transfers between devices, shift(): lax.ppermute(array, axis, [(i, (i + by) % count) for i in range(count)])  14.4 us
    ppermute x6, starting transfers between devices, shift(): lax.ppermute(array, axis, [(i, (i + by) % count) for i in range(count)])  12.5 us
    pallas_call x1, Pallas kernels, on_device(): pl.pallas_call(body, out_shape=[shape((K, atoms, chans), F32), shape((K,...  11.7 us
    pallas_call x1, Pallas kernels, on_device(): pl.pallas_call(table_kernel, out_shape=[shape((N_ROWS, edges, chans), F32...  9.18 us
    pallas_call x1, Pallas kernels, on_device(): pl.pallas_call(update_kernel, out_shape=shape((K, atoms, group), BF16), i...  2.84 us
  transfers between devices with their start and end apart: 6, of which 4 were waited for; matrix products, arithmetic and copies ran while one was open for 0% of the time, Pallas kernels for 17%

commit v1 on v0

v1 whole, which is shorter than its diff:
```python
import functools

import jax
import jax.numpy as jnp
from jax import lax
from jax.experimental import pallas as pl
from jax.experimental.pallas import tpu as pltpu
from jax.sharding import PartitionSpec as P

HEADS = 8
LMAX = 6
MMAX = 2
F32 = jnp.float32
BF16 = jnp.bfloat16
HIGH = lax.Precision.HIGHEST
NT = (((1,), (1,)), ((), ()))
NN = (((1,), (0,)), ((), ()))
TN = (((0,), (0,)), ((), ()))
BLOCK = 16


def dot(a, b, dims=NN, precision=None):
    return lax.dot_general(a, b, dims, precision=precision, preferred_element_type=F32)


def kept_rows():
    rows = {}
    offset = 0
    for level in range(LMAX + 1):
        width = 2 * level + 1
        reach = min(level, MMAX)
        for order in range(-reach, reach + 1):
            rows[level, order] = offset + (level + order) * width
        offset += width * width
    return rows


ROWS = kept_rows()
K = (LMAX + 1) ** 2


def vmem(n):
    return [pl.BlockSpec(memory_space=pltpu.VMEM)] * n


def hbm():
    return pl.BlockSpec(memory_space=pltpu.MemorySpace.HBM)


def pinned(array):
    return pltpu.with_memory_space_constraint(array, pltpu.MemorySpace.HBM)


def params(mib):
    return pltpu.CompilerParams(vmem_limit_bytes=mib * 1024 * 1024)


def iota(shape, axis):
    return lax.broadcasted_iota(jnp.int32, shape, axis)


def ones_where(mask):
    return jnp.where(mask, 1.0, 0.0).astype(F32)


def same_atom(atoms, edges):
    return ones_where(lax.rem(iota((atoms, edges), 1), atoms) == iota((atoms, edges), 0))


def edge_row(table):
    slots, atoms = table.shape
    edges = slots * atoms
    spread = dot(table.astype(F32), same_atom(atoms, edges), precision=HIGH)
    mine = lax.div(iota((slots, edges), 1), atoms) == iota((slots, edges), 0)
    return jnp.sum(jnp.where(mine, spread, 0.0), axis=0, keepdims=True)


def to_column(row):
    n = row.shape[1]
    return jnp.sum(jnp.where(iota((n, n), 0) == iota((n, n), 1), row, 0.0), axis=1, keepdims=True)


def onehot(row, height):
    return ones_where(iota((height, row.shape[1]), 0).astype(F32) == row)


def side(array, axis):
    return jnp.concatenate(array, axis=axis)


def paired(value):
    zero = jnp.zeros_like(value)
    return side([side([value, zero], 1), side([zero, value], 1)], 0)


def entry(dtab, row):
    one = dtab[pl.ds(row, 8, stride=0), :]
    return side([one] * (BLOCK // 8), 0)


def rotate_in(block, feats, dtab, store):
    here = pl.ds(pl.multiple_of(block * BLOCK, BLOCK), BLOCK)
    for level in range(LMAX + 1):
        width = 2 * level + 1
        planes = [feats[level * level + col, here, :] for col in range(width)]
        reach = min(level, MMAX)
        for order in range(-reach, reach + 1):
            first = ROWS[level, order]
            acc = entry(dtab, first) * planes[0]
            for col in range(1, width):
                acc = acc + entry(dtab, first + col) * planes[col]
            store(level, order, acc)


def rotate_out(block, load, dtab, store):
    here = pl.ds(pl.multiple_of(block * BLOCK, BLOCK), BLOCK)
    for level in range(LMAX + 1):
        reach = min(level, MMAX)
        orders = range(-reach, reach + 1)
        planes = {order: load(level, order) for order in orders}
        for col in range(2 * level + 1):
            acc = None
            for order in orders:
                term = entry(dtab, ROWS[level, order] + col) * planes[order]
                acc = term if acc is None else acc + term
            store(level * level + col, here, acc)


def rows_at(level, least, height, block):
    return pl.ds(pl.multiple_of((level - least) * height + block * BLOCK, BLOCK), BLOCK)


def place(order, level, height, block):
    least = abs(order)
    return least, rows_at(level, least, height, block), 1 if order < 0 else 0


def joined(ref, chans):
    count, group = ref.shape[-3], ref.shape[-2]
    if len(ref.shape) == 4:
        return [ref[:, level].reshape(count * group, chans) for level in range(count)]
    return [ref[:, :, level].reshape(2 * count * group, chans) for level in range(count)]


def table_kernel(
    after, wigner_hbm, rotation_hbm, w0_hbm, w1_hbm, w2_hbm,
    dtab, w0, w1, w2, t0, t1, t2,
    wigner, rotation, sems,
):
    copies = [
        pltpu.make_async_copy(source, target, sems.at[at])
        for at, (source, target) in enumerate(
            [
                (rotation_hbm, rotation), (wigner_hbm, wigner),
                (w0_hbm, w0), (w1_hbm, w1), (w2_hbm, w2),
            ]
        )
    ]
    for copy in copies:
        copy.start()
    copies[0].wait()
    pick = onehot(edge_row(rotation[...]), wigner.shape[1]).astype(BF16)
    copies[1].wait()
    wig = wigner[...]
    high = wig.astype(BF16)
    rest = wig - high.astype(F32)
    mid = rest.astype(BF16)
    low = (rest - mid.astype(F32)).astype(BF16)
    dtab[...] = dot(high, pick) + dot(mid, pick) + dot(low, pick)
    for copy, ref, out in zip(copies[2:], (w0, w1, w2), (t0, t1, t2)):
        copy.wait()
        chans = ref.shape[-1]
        for level, part in enumerate(joined(ref, chans)):
            out[level * chans : (level + 1) * chans, :] = jnp.transpose(part)


def fetch(rows_of, pick, feats):
    edges = pick.shape[1]
    group = feats.shape[1]
    both = paired(pick).astype(BF16)
    pairs = (K + 1) // 2
    for first in range(0, pairs, 2):
        blocks = [first, min(first + 1, pairs - 1)]
        got = dot(side([rows_of(at) for at in blocks], 0), both, TN)
        for lane, at in enumerate(blocks):
            for row in range(2):
                if 2 * at + row < K:
                    feats[2 * at + row] = got[
                        row * group : (row + 1) * group, lane * edges : (lane + 1) * edges
                    ]


def start_kernel(own, ghosts, source, grad_hbm, dtab, g0, g1, g2, r0, r1, r2, out_grad, feats, held, sem):
    copy = pltpu.make_async_copy(grad_hbm, out_grad, sem)
    copy.start()
    slots, atoms = source.shape
    edges = slots * atoms
    group = out_grad.shape[2]
    pick = onehot(edge_row(source[...]), atoms + ghosts.shape[1])
    fetch(lambda at: side([own[at], ghosts[at]], 0), pick, feats)
    copy.wait()
    both = paired(same_atom(atoms, edges)).astype(BF16)
    for first in range(0, K, 2):
        ks = [first, min(first + 1, K - 1)]
        got = dot(side([out_grad[k] for k in ks], 0), both, TN)
        for at, k in enumerate(ks):
            held[k] = got[:, at * edges : (at + 1) * edges]

    def step(block, carry):
        for values, outs, kind in ((feats, (r0, r1, r2), BF16), (held, (g0, g1, g2), F32)):

            def store(level, order, acc, outs=outs, kind=kind):
                which, rows, half = place(order, level, group, block)
                outs[which][rows, half * edges : (half + 1) * edges] = acc.astype(kind)

            rotate_in(block, values, dtab, store)
        return carry

    lax.fori_loop(0, group // BLOCK, step, 0)


def over_slots(value, slots, combine):
    edges = value.shape[1]
    out = value
    for slot in range(1, slots):
        out = combine(out, pltpu.roll(value, slot * (edges // slots), axis=1))
    return out


def head_sums(value, heads):
    width = value.shape[0] // heads
    sums = [
        jnp.sum(value[at * width : (at + 1) * width], axis=0, keepdims=True) for at in range(heads)
    ]
    return side(sums + [jnp.zeros_like(sums[0])] * (-heads % 8), 0)


def head_spread(value, heads, width):
    return side(
        [jnp.broadcast_to(value[at : at + 1], (width, value.shape[1])) for at in range(heads)], 0
    )


def edge_kernel(heads, shards, *refs):
    own_parts, ghost_parts, refs = refs[: shards - 1], refs[shards - 1 : 2 * shards - 2], refs[2 * shards - 2 :]
    p0, p1, p2, source, counts, dtab, g0, g1, g2, w0, w1, w2, t0, t1, t2, attn, *refs = refs
    own_out, a_out, b_out, v0, v1, v2, feats, r0, r1, r2, d0, d1, d2, dfeats = refs
    slots, atoms = source.shape
    edges = slots * atoms
    chans = w0.shape[-1]
    group = w0.shape[2]
    half = a_out.shape[1]
    table = atoms + 2 * half
    me = lax.axis_index("ch")
    rots = (r0, r1, r2)
    sources = edge_row(source[...])
    pick = onehot(sources, table)

    for least, (ref, part) in enumerate(zip(rots, (p0, p1, p2))):
        for at in range(LMAX + 1 - least):
            there = pl.ds(pl.multiple_of(at * chans + me * group, BLOCK), group)
            ref[there, :] = part[at * group : (at + 1) * group, :]

    for step, (own, ghosts) in enumerate(zip(own_parts, ghost_parts), 1):
        fetch(lambda at: side([own[at], ghosts[at]], 0), pick, feats)
        base = lax.rem(me + step, shards) * group

        def in_step(block, carry):
            def store(level, order, acc):
                least = abs(order)
                lane = edges if order < 0 else 0
                row = (level - least) * chans + base + block * BLOCK
                rots[least][pl.ds(pl.multiple_of(row, BLOCK), BLOCK), lane : lane + edges] = acc.astype(BF16)

            rotate_in(block, feats, dtab, store)
            return carry

        lax.fori_loop(0, group // BLOCK, in_step, 0)

    def weights_of(ref):
        return side(joined(ref, chans), 1)

    y0 = dot(weights_of(w0), r0[...])

    def mixed(ref, rot):
        out = dot(weights_of(ref), rot[...])
        tall = out.shape[0] // 2
        plus = out[:tall, :edges] - out[tall:, edges:]
        minus = out[:tall, edges:] + out[tall:, :edges]
        return side([plus, minus], 1)

    mixes = (y0, mixed(w1, r1), mixed(w2, r2))
    grads = (g0[...], g1[...], g2[...])

    scalar = y0[:group]
    sig = 1.0 / (1.0 + jnp.exp(-scalar))
    vector = to_column(attn[...])
    width = group // heads
    spread = dot(counts[...].astype(F32), same_atom(atoms, edges), precision=HIGH)
    score = head_sums(scalar * sig * vector, heads)
    live = lax.div(iota(score.shape, 1), atoms).astype(F32) < spread
    score = jnp.where(live, score, -1e30)
    top = over_slots(score, slots, jnp.maximum)
    weight = jnp.where(live, jnp.exp(score - top), 0.0)
    weight = weight / over_slots(weight, slots, jnp.add)
    factor = head_spread(weight, heads, width) * sig

    overlap = None
    for grad, mix in zip(grads, mixes):
        product = grad * mix
        for at in range(0, product.shape[0], group):
            for lane in range(0, product.shape[1], edges):
                piece = product[at : at + group, lane : lane + edges]
                overlap = piece if overlap is None else overlap + piece
    dweight = head_sums(overlap * sig, heads)
    mean = over_slots(weight * dweight, slots, jnp.add)
    dscore = head_spread(weight * (dweight - mean), heads, width)
    dscalar = overlap * factor * (1.0 - sig) + dscore * vector * sig * (1.0 + scalar * (1.0 - sig))

    dmix = []
    for grad, mix, out in zip(grads, mixes, (v0, v1, v2)):
        wide = side([factor] * (mix.shape[1] // edges), 1)
        wide = side([wide] * (mix.shape[0] // group), 0)
        out[...] = mix * wide
        dmix.append(grad * wide)
    back0 = side([dmix[0][:group] + dscalar, dmix[0][group:]], 0).astype(BF16)
    d0[...] = dot(t0[...], back0).astype(BF16).astype(F32)
    for ref, value, out in ((t1, dmix[1], d1), (t2, dmix[2], d2)):
        flipped = side([value[:, edges:], -value[:, :edges]], 1)
        stacked = side([value, flipped], 0).astype(BF16)
        out[...] = dot(ref[...], stacked).astype(BF16).astype(F32)

    drots = (d0, d1, d2)

    def out_step(block, carry):
        def load(level, order):
            which, rows, side_no = place(order, level, chans, block)
            return drots[which][rows, side_no * edges : (side_no + 1) * edges]

        def store(k, here, value):
            dfeats[k, here, :] = value.astype(BF16)

        rotate_out(block, load, dtab, store)
        return carry

    lax.fori_loop(0, chans // BLOCK, out_step, 0)

    numbers = sources.astype(jnp.int32)
    turned = atoms + lax.rem(numbers - atoms + parity() * half, 2 * half)
    pick = onehot(jnp.where(numbers < atoms, numbers, turned).astype(F32), table).astype(BF16)
    for first in range(0, K, 2):
        ks = [k for k in (first, first + 1) if k < K]
        got = dot(pick, side([dfeats[k] for k in ks], 0), NT)
        for at, k in enumerate(ks):
            mine = got[:, at * chans : (at + 1) * chans]
            own_out[k] = mine[:atoms]
            a_out[k] = mine[atoms : atoms + half].astype(BF16)
            b_out[k] = mine[atoms + half :].astype(BF16)


def update_kernel(v0, v1, v2, dtab, mine, out, back):
    atoms, group = mine.shape[1], mine.shape[2]
    edges = dtab.shape[1]
    values = (v0, v1, v2)

    def step(block, carry):
        def load(level, order):
            which, rows, side_no = place(order, level, group, block)
            return values[which][rows, side_no * edges : (side_no + 1) * edges]

        def store(k, here, value):
            back[k, here, :] = value.astype(BF16)

        rotate_out(block, load, dtab, store)
        return carry

    lax.fori_loop(0, group // BLOCK, step, 0)
    owner = same_atom(atoms, edges).astype(BF16)
    for k in range(K):
        agg = dot(owner, back[k], NT)
        out[k] = (mine[k].astype(F32) + agg).astype(BF16)


def parity():
    return lax.rem(lax.axis_index("dom"), 2)


def pack_kernel(mine_hbm, ghost_hbm, out, mine, ghost, sems):
    copies = [
        pltpu.make_async_copy(mine_hbm, mine, sems.at[0]),
        pltpu.make_async_copy(ghost_hbm, ghost, sems.at[1]),
    ]
    for copy in copies:
        copy.start()
    for copy in copies:
        copy.wait()
    for at in range(out.shape[0] - 1):
        out[at] = side([mine[2 * at], mine[min(2 * at + 1, K - 1)]], 1)
    slots = ghost[...].astype(F32)
    rest = jnp.zeros((1, out.shape[2] - slots.shape[1]), F32)
    out[out.shape[0] - 1] = jnp.broadcast_to(side([slots, rest], 1), out.shape[1:]).astype(BF16)


def ghost_kernel(after, first, second, ghost, out):
    atoms = first.shape[1]
    slots = ghost.shape[1]
    odd = parity()
    lane = iota((1, slots), 1)
    target = ghost[...] + jnp.where(lane < slots // 2, odd * atoms, (1 - odd) * atoms)
    rows = to_column(target.astype(F32))
    pick = ones_where(iota((slots, 2 * atoms), 1).astype(F32) == rows).astype(BF16)
    for at in range(out.shape[0]):
        out[at] = dot(pick, side([first[at], second[at]], 0)).astype(BF16)


def settle_kernel(shards, own, got_a, got_b, face_a, face_b, out_grad, mine_out, *others):
    group = out_grad.shape[2]
    atoms, chans = own.shape[1:]
    half = got_a.shape[1]
    me = lax.axis_index("ch")
    even = parity() == 0
    slots_a = face_a[face_a.shape[0] - 1][:, : 2 * half].astype(F32)
    slots_b = face_b[face_b.shape[0] - 1][:, : 2 * half].astype(F32)
    asked = side(
        [
            jnp.where(even, slots_a[:, half:], slots_a[:, :half]),
            jnp.where(even, slots_b[:, :half], slots_b[:, half:]),
        ],
        1,
    )
    pick = ones_where(asked == iota((atoms, 2 * half), 0).astype(F32)).astype(BF16)

    def part(value, step):
        wanted = lax.rem(me + step, shards)
        out = value[:, :group]
        for chunk in range(1, shards):
            out = jnp.where(wanted == chunk, value[:, chunk * group : (chunk + 1) * group], out)
        return out

    for first in range(0, K, 2):
        ks = [first, min(first + 1, K - 1)]
        ghosts = side([side([got_a[k], got_b[k]], 0) for k in ks], 1)
        got = dot(pick, ghosts)
        totals = [own[k] + got[:, at * chans : (at + 1) * chans] for at, k in enumerate(ks)]
        for k, total in zip(ks, totals):
            mine_out[k] = part(total, 0) + out_grad[k].astype(F32)
        for step in range(1, shards):
            others[step - 1][first // 2] = side(
                [part(total, step) for total in totals], 1
            ).astype(BF16)


def final_kernel(mine, *refs):
    others, out = refs[:-1], refs[-1]
    group = mine.shape[2]
    for k in range(K):
        lane = (k % 2) * group
        total = mine[k]
        for other in others:
            total = total + other[k // 2].astype(F32)[:, lane : lane + group]
        out[k] = total


def shift(array, axis, by):
    count = lax.axis_size(axis)
    return lax.ppermute(array, axis, [(i, (i + by) % count) for i in range(count)])


def swap(array, first):
    count = lax.axis_size("dom")
    step = [-1, 1] if first else [1, -1]
    return lax.ppermute(array, "dom", [(i, (i + step[i % 2]) % count) for i in range(count)])


def cost(flops, size):
    return pl.CostEstimate(flops=flops, bytes_accessed=size, transcendentals=0)


def on_device(
    node_irreps, out_grad, edge_source, edge_rotation, edge_count, ghost_slot, wigner,
    so2_m0, so2_m1, so2_m2, attn_vector,
):
    group, atoms = node_irreps.shape[1], node_irreps.shape[2]
    shards = lax.axis_size("ch")
    chans = group * shards
    slots = edge_source.shape[0]
    edges = slots * atoms
    heads_here = HEADS // shards
    shape = jax.ShapeDtypeStruct
    mine = jnp.transpose(node_irreps, (0, 2, 1))
    grad = jnp.transpose(out_grad, (0, 2, 1))
    w0 = jnp.transpose(so2_m0, (0, 2, 1, 3))
    w1 = jnp.transpose(so2_m1, (0, 1, 3, 2, 4))
    w2 = jnp.transpose(so2_m2, (0, 1, 3, 2, 4))

    pairs = (K + 1) // 2
    ghosts = ghost_slot.reshape(1, -1)
    half = ghosts.shape[1] // 2
    packed = pl.pallas_call(
        pack_kernel,
        out_shape=shape((pairs + 1, atoms, 2 * group), BF16),
        in_specs=[hbm(), hbm()],
        out_specs=vmem(1)[0],
        scratch_shapes=[
            pltpu.VMEM(mine.shape, BF16),
            pltpu.VMEM(ghosts.shape, jnp.int32),
            pltpu.SemaphoreType.DMA((2,)),
        ],
        compiler_params=params(4),
        name="pack",
    )(pinned(mine), pinned(ghosts))
    face_a = swap(packed, True)
    others = [shift(packed, "ch", -step) for step in range(1, shards)]
    face_b = swap(packed, False)

    shapes = [
        ((LMAX + 1 - least) * group, edges * (1 if least == 0 else 2)) for least in range(MMAX + 1)
    ]
    wide = [
        ((LMAX + 1 - least) * chans, edges * (1 if least == 0 else 2)) for least in range(MMAX + 1)
    ]
    weights = (w0, w1, w2)
    turned = [(wide[i][0], shapes[i][0] * (2 if i else 1)) for i in range(3)]
    dtab, *tables = pl.pallas_call(
        table_kernel,
        out_shape=[shape((wigner.shape[0], edges), F32)]
        + [shape(w.shape, BF16) for w in weights]
        + [shape(t, BF16) for t in turned],
        in_specs=[hbm()] * 6,
        out_specs=vmem(7),
        scratch_shapes=[
            pltpu.VMEM(wigner.shape, F32),
            pltpu.VMEM(edge_rotation.shape, jnp.int32),
            pltpu.SemaphoreType.DMA((5,)),
        ],
        compiler_params=params(16),
        cost_estimate=cost(20_000_000, 4_000_000),
        name="tables",
    )(packed, pinned(wigner), pinned(edge_rotation), *[pinned(w) for w in weights])
    weights, turned = tables[:3], tables[3:]

    ghost_mine = pl.pallas_call(
        ghost_kernel,
        out_shape=shape((pairs, 2 * half, 2 * group), BF16),
        in_specs=[hbm(), *vmem(3)],
        out_specs=vmem(1)[0],
        compiler_params=params(4),
        name="ghosts",
    )(dtab, face_a, face_b, ghosts)
    ghost_others = [shift(ghost_mine, "ch", -step) for step in range(1, shards)]

    own_rows = [(shapes[i][0], shapes[i][1]) for i in range(3)]
    started = pl.pallas_call(
        start_kernel,
        out_shape=[shape(s, F32) for s in shapes]
        + [shape(s, BF16) for s in own_rows]
        + [shape(grad.shape, BF16)],
        in_specs=[*vmem(3), hbm(), *vmem(1)],
        out_specs=vmem(7),
        scratch_shapes=[
            pltpu.VMEM((K, group, edges), F32),
            pltpu.VMEM((K, group, edges), F32),
            pltpu.SemaphoreType.DMA(()),
        ],
        compiler_params=params(16),
        cost_estimate=cost(20_000_000, 4_000_000),
        name="start",
    )(packed, ghost_mine, edge_source, pinned(grad), dtab)
    grads, rotated, grad = started[:3], started[3:6], started[6]

    own, to_a, to_b, *values = pl.pallas_call(
        functools.partial(edge_kernel, heads_here, shards),
        out_shape=[
            shape((K, atoms, chans), F32),
            shape((K, half, chans), BF16),
            shape((K, half, chans), BF16),
        ] + [shape(s, F32) for s in shapes],
        in_specs=vmem(14 + 2 * shards),
        out_specs=vmem(6),
        scratch_shapes=[pltpu.VMEM((K, group, edges), F32)]
        + [pltpu.VMEM(s, BF16) for s in wide]
        + [pltpu.VMEM(s, F32) for s in wide]
        + [pltpu.VMEM((K, chans, edges), BF16)],
        compiler_params=params(24),
        cost_estimate=cost(2_000_000_000, 20_000_000),
        name="edges",
    )(
        *others, *ghost_others, *rotated, edge_source, edge_count.reshape(1, -1),
        dtab, *grads, *weights, *turned, attn_vector.reshape(1, -1),
    )
    got_a = swap(to_a, True)
    got_b = swap(to_b, False)

    updated = pl.pallas_call(
        update_kernel,
        out_shape=shape((K, atoms, group), BF16),
        in_specs=vmem(5),
        out_specs=vmem(1)[0],
        scratch_shapes=[pltpu.VMEM((K, group, edges), BF16)],
        compiler_params=params(8),
        cost_estimate=cost(20_000_000, 4_000_000),
        name="update",
    )(*values, dtab, mine)

    mine_grad, *sent = pl.pallas_call(
        functools.partial(settle_kernel, shards),
        out_shape=[shape((K, atoms, group), F32)]
        + [shape((pairs, atoms, 2 * group), BF16)] * (shards - 1),
        in_specs=vmem(6),
        out_specs=vmem(shards),
        compiler_params=params(8),
        name="settle",
    )(own, got_a, got_b, face_a, face_b, grad)
    mine_grad = pl.pallas_call(
        final_kernel,
        out_shape=shape((K, atoms, group), F32),
        in_specs=vmem(shards),
        out_specs=vmem(1)[0],
        compiler_params=params(4),
        name="final",
    )(mine_grad, *[shift(sent[step - 1], "ch", step) for step in range(1, shards)])
    return (jnp.transpose(updated, (0, 2, 1)), jnp.transpose(mine_grad, (0, 2, 1)))


def solution(mesh):
    placed = (
        P(None, "ch", "dom"), P(None, "ch", "dom"), P(None, "dom"), P(None, "dom"), P("dom"),
        P("dom"), P(None, "dom"), P(None, "ch", None, None), P(None, None, "ch", None, None),
        P(None, None, "ch", None, None), P("ch"),
    )
    return jax.shard_map(
        on_device,
        mesh=mesh,
        in_specs=placed,
        out_specs=(P(None, "ch", "dom"), P(None, "ch", "dom")),
        check_vma=False,
    )
```

time: 69.4 us -> 35.2 us (0.51)
  local copies, waits for them, and re-layouts: 16.3 us -> 0.02 us
  Pallas kernels: 24.3 us -> 14.6 us
  waiting for transfers between devices: 14.4 us -> 8.75 us
  starting transfers between devices: 12.5 us -> 11 us
  other arithmetic: 0.8 us -> 0 us
    unnamed x30 -> x10, local copies, waits for them, and re-layouts: 16.3 us -> 0.02 us
    ppermute x6 -> x3, waiting for transfers between devices: 14.4 us -> 4.01 us  [shift(): lax.ppermute(array, axis, [(i, (i + by) % count) for i in range(count)])]
    ppermute x6 -> x3, starting transfers between devices: 12.5 us -> 2.69 us  [shift(): lax.ppermute(array, axis, [(i, (i + by) % count) for i in range(count)])]
    pallas_call x3 -> x6, Pallas kernels: 21.1 us -> 12.3 us  [the longest x1 5.23 us: on_device(): pl.pallas_call(functools.partial(edge_kernel, heads_here, shards), out_sh...]
    ppermute x0 -> x4, starting transfers between devices: none -> 8.29 us  [swap(): lax.ppermute(array, 'dom', [(i, (i + step[i % 2]) % count) for i in range...]
    ppermute x0 -> x4, waiting for transfers between devices: none -> 4.74 us  [swap(): lax.ppermute(array, 'dom', [(i, (i + step[i % 2]) % count) for i in range...]
    pallas_call x1, Pallas kernels: 2.84 us -> 1.72 us  [on_device(): pl.pallas_call(update_kernel, out_shape=shape((K, atoms, group), BF16), i...]
    transpose x1 -> x0, other arithmetic: 0.8 us -> none  [on_device(): jnp.transpose(mine_grad, (0, 2, 1))]
  transfers between devices with their start and end apart: 6 -> 7, of which waited for: 4 -> 3; matrix products, arithmetic and copies ran while one was open for 0% -> 0% of each run, Pallas kernels for 17% -> 20%
where the time goes in v1:
time: 35.2 us; the launch traced here: 35.1 us
  Pallas kernels  14.6 us (41%)
  starting transfers between devices  11 us (31%)
  waiting for transfers between devices  8.75 us (25%)
  between operations  0.72 us (2%)
    ppermute x4, starting transfers between devices, swap(): lax.ppermute(array, 'dom', [(i, (i + step[i % 2]) % count) for i in range...  8.29 us
    pallas_call x1, Pallas kernels, on_device(): pl.pallas_call(functools.partial(edge_kernel, heads_here, shards), out_sh...  5.23 us
    ppermute x4, waiting for transfers between devices, swap(): lax.ppermute(array, 'dom', [(i, (i + step[i % 2]) % count) for i in range...  4.74 us
    ppermute x3, waiting for transfers between devices, shift(): lax.ppermute(array, axis, [(i, (i + by) % count) for i in range(count)])  4.01 us
    ppermute x3, starting transfers between devices, shift(): lax.ppermute(array, axis, [(i, (i + by) % count) for i in range(count)])  2.69 us
    pallas_call x1, Pallas kernels, on_device(): pl.pallas_call(start_kernel, out_shape=[shape(s, F32) for s in shapes] +...  2.5 us
    pallas_call x1, Pallas kernels, on_device(): pl.pallas_call(table_kernel, out_shape=[shape((wigner.shape[0], edges), F...  2.39 us
    pallas_call x1, Pallas kernels, on_device(): pl.pallas_call(update_kernel, out_shape=shape((K, atoms, group), BF16), i...  1.72 us
  transfers between devices with their start and end apart: 7, of which 3 were waited for; matrix products, arithmetic and copies ran while one was open for 0% of the time, Pallas kernels for 20%

profile of v1, /device:TPU:0, one launch (start us, length us, event | category | flops | bytes accessed | tf_op | source)
XLA Modules:
  0.0 35.1 jit_solution(15712200856946119343)
XLA Ops:
  0.6 1.0 %pack.1.after.own = bf16[26,16,128]{2,1,0:T(8,128)(2,1)S(1)} custom-call(bf16[49,16,64]{2,1,0:T(8,128)(2,1)} %bitcast.10, s32[1,16]{1,0:T(1,128)} %bitcast.12), custom_call_target="tpu_custom_call" | custom-call | tf_op jit(solution)/shard_map/pack/pallas_call | solution.py:499
  1.7 0.6 %collective-permute-start.2 = (bf16[26,16,128]{2,1,0:T(8,128)(2,1)S(1)}, bf16[26,16,128]{2,1,0:T(8,128)(2,1)S(1)}, u32[]{:S(2)}, u32[]{:S(2)}) collective-permute-start(bf16[26,16,128]{2,1,0:T(8,128)(2,1)S(1)} %pack.1.after.own), channel_id=1, source_target_pairs={{0,2},{2,0},{4,6},{6,4},{8,10},{10,8},{12,14},{14,12},{16,18},{18,... | collective-permute-start | bytes 319496 | tf_op jit(solution)/shard_map/ppermute | solution.py:472
  2.2 5.7 %collective-permute-start.1 = (bf16[26,16,128]{2,1,0:T(8,128)(2,1)S(1)}, bf16[26,16,128]{2,1,0:T(8,128)(2,1)S(1)}, u32[]{:S(2)}, u32[]{:S(2)}) collective-permute-start(bf16[26,16,128]{2,1,0:T(8,128)(2,1)S(1)} %pack.1.after.own), channel_id=1, source_target_pairs={{0,30},{2,4},{4,2},{6,8},{8,6},{10,12},{12,10},{14,16},{16,14},{18... | collective-permute-start | bytes 319496 | tf_op jit(solution)/shard_map/ppermute | solution.py:472
  7.9 1.5 %collective-permute-start = (bf16[26,16,128]{2,1,0:T(8,128)(2,1)S(1)}, bf16[26,16,128]{2,1,0:T(8,128)(2,1)S(1)}, u32[]{:S(2)}, u32[]{:S(2)}) collective-permute-start(bf16[26,16,128]{2,1,0:T(8,128)(2,1)S(1)} %pack.1.after.own), channel_id=1, source_target_pairs={{0,1},{1,0},{2,3},{3,2},{4,5},{5,4},{6,7},{7,6},{8,9},{9,8},{10,11... | collective-permute-start | bytes 319496 | tf_op jit(solution)/shard_map/ppermute | solution.py:466
  9.4 2.4 %tables.1 = (f32[455,128]{1,0:T(8,128)S(1)}, bf16[7,7,64,128]{3,2,1,0:T(8,128)(2,1)S(1)}, bf16[2,6,6,64,128]{4,3,2,1,0:T(8,128)(2,1)S(1)}, bf16[2,5,5,64,128]{4,...) custom-call(bf16[26,16,128]{2,1,0:T(8,128)(2,1)S(1)} %pack.1.after.o, ...), custom_call_target="tpu_custom_call" | custom-call | flops 20000000 | bytes 4000000 | tf_op jit(solution)/shard_map/tables/pallas_call | solution.py:524
  11.8 0.0 copy-start.3
  11.8 0.0 copy-start.4
  11.8 0.0 collective-permute-done.2.second.face_b
  11.8 0.0 collective-permute-done.1.first.face_a
  11.8 0.3 ghosts.1
  12.1 0.6 %collective-permute-start.3 = (bf16[25,16,128]{2,1,0:T(8,128)(2,1)S(1)}, bf16[25,16,128]{2,1,0:T(8,128)(2,1)S(1)}, u32[]{:S(2)}, u32[]{:S(2)}) collective-permute-start(bf16[25,16,128]{2,1,0:T(8,128)(2,1)S(1)} %ghosts.1), channel_id=1, source_target_pairs={{0,1},{1,0},{2,3},{3,2},{4,5},{5,4},{6,7},{7,6},{8,9},{9,8},{10,11... | collective-permute-start | bytes 307208 | tf_op jit(solution)/shard_map/ppermute | solution.py:466
  12.7 2.5 %start.1 = (f32[448,128]{1,0:T(8,128)S(1)}, f32[384,256]{1,0:T(8,128)S(1)}, f32[320,256]{1,0:T(8,128)S(1)}, bf16[448,128]{1,0:T(8,128)(2,1)S(1)}, bf16[384,256]{...) custom-call(bf16[26,16,128]{2,1,0:T(8,128)(2,1)S(1)} %pack.1.after.own, ...), custom_call_target="tpu_custom_call" | custom-call | flops 20000000 | bytes 4000000 | tf_op jit(solution)/shard_map/start/pallas_call | solution.py:553
  15.2 0.0 collective-permute-done.refs_0_
  15.3 1.6 %collective-permute-done.3.refs_1_ = bf16[25,16,128]{2,1,0:T(8,128)(2,1)S(1)} collective-permute-done((bf16[25,16,128]{2,1,0:T(8,128)(2,1)S(1)}, bf16[25,16,128]{2,1,0:T(8,128)(2,1)S(1)}, u32[]{:S(2)}, u32[]{:S(2)}) %collective-permute-start.3) | collective-permute-done | bytes 102432 | tf_op jit(solution)/shard_map/ppermute | solution.py:466
  16.9 5.2 %edges.1 = (f32[49,16,128]{2,1,0:T(8,128)S(1)}, bf16[49,8,128]{2,1,0:T(8,128)(2,1)S(1)}, bf16[49,8,128]{2,1,0:T(8,128)(2,1)S(1)}, f32[448,128]{1,0:T(8,128)S(1)}...) custom-call(bf16[26,16,128]{2,1,0:T(8,128)(2,1)S(1)} %collective-permute-done.refs_0_, ...), custom_call_target="tpu_custom_call" | custom-call | flops 2000000000 | bytes 20000000 | tf_op jit(solution)/shard_map/edges/pallas_call | solution.py:571
  22.1 2.1 %collective-permute-start.4 = (bf16[49,8,128]{2,1,0:T(8,128)(2,1)S(1)}, bf16[49,8,128]{2,1,0:T(8,128)(2,1)S(1)}, u32[]{:S(2)}, u32[]{:S(2)}) collective-permute-start(bf16[49,8,128]{2,1,0:T(8,128)(2,1)S(1)} %get-tuple-element.41), channel_id=1, source_target_pairs={{0,30},{2,4},{4,2},{6,8},{8,6},{10,12},{12,10},{14,16},{16,14},{18... | collective-permute-start | bytes 301064 | tf_op jit(solution)/shard_map/ppermute | solution.py:472
  24.2 0.0 collective-permute-start.5
  24.2 4.7 %collective-permute-done.4.got_a = bf16[49,8,128]{2,1,0:T(8,128)(2,1)S(1)} collective-permute-done((bf16[49,8,128]{2,1,0:T(8,128)(2,1)S(1)}, bf16[49,8,128]{2,1,0:T(8,128)(2,1)S(1)}, u32[]{:S(2)}, u32[]{:S(2)}) %collective-permute-start.4) | collective-permute-done | bytes 100384 | tf_op jit(solution)/shard_map/ppermute | solution.py:472
  28.9 0.0 collective-permute-done.5.got_b
  28.9 0.6 %settle.1 = (f32[49,16,64]{2,1,0:T(8,128)S(1)}, bf16[25,16,128]{2,1,0:T(8,128)(2,1)S(1)}) custom-call(f32[49,16,128]{2,1,0:T(8,128)S(1)} %get-tuple-element.40.own, bf16[49,8,128]{2,1,0:T(8,128)(2,1)S(1)} %collective-permute-done.4.got_a, bf16[49,8,128]{2,1,0:T(8,128)(2,1)S(1)} %collective-permute-done.5.got_b, ...), custom_call_target="tpu_custom_call" | custom-call | tf_op jit(solution)/shard_map/settle/pallas_call | solution.py:605
  29.5 0.6 %collective-permute-start.6 = (bf16[25,16,128]{2,1,0:T(8,128)(2,1)S(1)}, bf16[25,16,128]{2,1,0:T(8,128)(2,1)S(1)}, u32[]{:S(2)}, u32[]{:S(2)}) collective-permute-start(bf16[25,16,128]{2,1,0:T(8,128)(2,1)S(1)} %get-tuple-element.45), channel_id=1, source_target_pairs={{0,1},{1,0},{2,3},{3,2},{4,5},{5,4},{6,7},{7,6},{8,9},{9,8},{10,11... | collective-permute-start | bytes 307208 | tf_op jit(solution)/shard_map/ppermute | solution.py:466
  30.1 1.7 %update.1 = bf16[49,16,64]{2,1,0:T(8,128)(2,1)} custom-call(f32[448,128]{1,0:T(8,128)S(1)} %get-tuple-element.37.v0, f32[384,256]{1,0:T(8,128)S(1)} %get-tuple-element.38.v1, f32[320,256]{1,0:T(8,128)S(1)} %get-tuple-element.39.v2, f32[455,128]{1,0:T(8,128)S(1)} %get-tuple-element.24.after.dtab.refs_7_, bf16[49,16,64]{2,1,0:T(8,128)(2,1)S(1)} %bitcast.11), custom_call_target="tpu_custom_call" | custom-call | flops 20000000 | bytes 4000000 | tf_op jit(solution)/shard_map/update/pallas_call | solution.py:594
  31.8 2.4 %collective-permute-done.6.refs_0_ = bf16[25,16,128]{2,1,0:T(8,128)(2,1)S(1)} collective-permute-done((bf16[25,16,128]{2,1,0:T(8,128)(2,1)S(1)}, bf16[25,16,128]{2,1,0:T(8,128)(2,1)S(1)}, u32[]{:S(2)}, u32[]{:S(2)}) %collective-permute-start.6) | collective-permute-done | bytes 102432 | tf_op jit(solution)/shard_map/ppermute | solution.py:466
  34.2 0.8 %final.1 = f32[49,16,64]{2,1,0:T(8,128)} custom-call(f32[49,16,64]{2,1,0:T(8,128)S(1)} %get-tuple-element.44.mine, bf16[25,16,128]{2,1,0:T(8,128)(2,1)S(1)} %collective-permute-done.6.refs_0_), custom_call_target="tpu_custom_call" | custom-call | tf_op jit(solution)/shard_map/final/pallas_call | solution.py:614
  (8 shorter events, 0.0 us)
Async XLA Ops:
  1.7 10.1 %collective-permute-start.2 = (bf16[26,16,128]{2,1,0:T(8,128)(2,1)S(1)}, bf16[26,16,128]{2,1,0:T(8,128)(2,1)S(1)}, u32[]{:S(2)}, u32[]{:S(2)}) collective-permute-start(bf16[26,16,128]{2,1,0:T(8,128)(2,1)S(1)} %pack.1.after.own), channel_id=1, source_target_pairs={{0,2},{2,0},{4,6},{6,4},{8,10},{10,8},{12,14},{14,12},{16,18},{18,... | collective-permute-start | bytes 319496 | tf_op jit(solution)/shard_map/ppermute | solution.py:472
  2.2 9.6 %collective-permute-start.1 = (bf16[26,16,128]{2,1,0:T(8,128)(2,1)S(1)}, bf16[26,16,128]{2,1,0:T(8,128)(2,1)S(1)}, u32[]{:S(2)}, u32[]{:S(2)}) collective-permute-start(bf16[26,16,128]{2,1,0:T(8,128)(2,1)S(1)} %pack.1.after.own), channel_id=1, source_target_pairs={{0,30},{2,4},{4,2},{6,8},{8,6},{10,12},{12,10},{14,16},{16,14},{18... | collective-permute-start | bytes 319496 | tf_op jit(solution)/shard_map/ppermute | solution.py:472
  7.9 7.3 %collective-permute-start = (bf16[26,16,128]{2,1,0:T(8,128)(2,1)S(1)}, bf16[26,16,128]{2,1,0:T(8,128)(2,1)S(1)}, u32[]{:S(2)}, u32[]{:S(2)}) collective-permute-start(bf16[26,16,128]{2,1,0:T(8,128)(2,1)S(1)} %pack.1.after.own), channel_id=1, source_target_pairs={{0,1},{1,0},{2,3},{3,2},{4,5},{5,4},{6,7},{7,6},{8,9},{9,8},{10,11... | collective-permute-start | bytes 319496 | tf_op jit(solution)/shard_map/ppermute | solution.py:466
  9.4 2.5 %copy-start.2 = (s32[16]{0:T(128)S(1)}, s32[16]{0:T(128)}, u32[]{:S(2)}) copy-start(s32[16]{0:T(128)} %param.16) | copy-start | bytes 196
  9.4 3.3 %copy-start.1 = (s32[8,16]{1,0:T(8,128)S(1)}, s32[8,16]{1,0:T(8,128)}, u32[]{:S(2)}) copy-start(s32[8,16]{1,0:T(8,128)} %refs_5_.1) | copy-start | bytes 1540
  11.8 5.1 %copy-start.3 = (s32[16]{0:T(128)S(1)}, s32[16]{0:T(128)}, u32[]{:S(2)}) copy-start(s32[16]{0:T(128)} %param.15) | copy-start | bytes 196
  11.8 5.1 %copy-start.4 = (f32[64]{0:T(128)S(1)}, f32[64]{0:T(128)}, u32[]{:S(2)}) copy-start(f32[64]{0:T(128)} %param.21) | copy-start | bytes 772
  12.1 4.7 %collective-permute-start.3 = (bf16[25,16,128]{2,1,0:T(8,128)(2,1)S(1)}, bf16[25,16,128]{2,1,0:T(8,128)(2,1)S(1)}, u32[]{:S(2)}, u32[]{:S(2)}) collective-permute-start(bf16[25,16,128]{2,1,0:T(8,128)(2,1)S(1)} %ghosts.1), channel_id=1, source_target_pairs={{0,1},{1,0},{2,3},{3,2},{4,5},{5,4},{6,7},{7,6},{8,9},{9,8},{10,11... | collective-permute-start | bytes 307208 | tf_op jit(solution)/shard_map/ppermute | solution.py:466
  16.9 13.2 %copy-start = (bf16[49,64,16]{1,2,0:T(8,128)(2,1)S(1)}, bf16[49,64,16]{1,2,0:T(8,128)(2,1)}, u32[]{:S(2)}) copy-start(bf16[49,64,16]{1,2,0:T(8,128)(2,1)} %param.11) | copy-start | bytes 301060
  22.1 6.8 %collective-permute-start.4 = (bf16[49,8,128]{2,1,0:T(8,128)(2,1)S(1)}, bf16[49,8,128]{2,1,0:T(8,128)(2,1)S(1)}, u32[]{:S(2)}, u32[]{:S(2)}) collective-permute-start(bf16[49,8,128]{2,1,0:T(8,128)(2,1)S(1)} %get-tuple-element.41), channel_id=1, source_target_pairs={{0,30},{2,4},{4,2},{6,8},{8,6},{10,12},{12,10},{14,16},{16,14},{18... | collective-permute-start | bytes 301064 | tf_op jit(solution)/shard_map/ppermute | solution.py:472
  24.2 4.7 %collective-permute-start.5 = (bf16[49,8,128]{2,1,0:T(8,128)(2,1)S(1)}, bf16[49,8,128]{2,1,0:T(8,128)(2,1)S(1)}, u32[]{:S(2)}, u32[]{:S(2)}) collective-permute-start(bf16[49,8,128]{2,1,0:T(8,128)(2,1)S(1)} %get-tuple-element.42), channel_id=1, source_target_pairs={{0,2},{2,0},{4,6},{6,4},{8,10},{10,8},{12,14},{14,12},{16,18},{18,... | collective-permute-start | bytes 301064 | tf_op jit(solution)/shard_map/ppermute | solution.py:472
  29.5 4.7 %collective-permute-start.6 = (bf16[25,16,128]{2,1,0:T(8,128)(2,1)S(1)}, bf16[25,16,128]{2,1,0:T(8,128)(2,1)S(1)}, u32[]{:S(2)}, u32[]{:S(2)}) collective-permute-start(bf16[25,16,128]{2,1,0:T(8,128)(2,1)S(1)} %get-tuple-element.45), channel_id=1, source_target_pairs={{0,1},{1,0},{2,3},{3,2},{4,5},{5,4},{6,7},{7,6},{8,9},{9,8},{10,11... | collective-permute-start | bytes 307208 | tf_op jit(solution)/shard_map/ppermute | solution.py:466
